TPU v7x, 32 devices: a 4x2x2 block of a 4x4x8 slice. The times are simulated.
32 devices in a mesh: dp: 4 (over y, z), sp: 8 (over x, core).
Axes of the slice: x: 4, y: 2, z: 2, core: 2. Of those that a mesh axis runs over, the one named last changes fastest.
The devices are a block of a 4x4x8 slice.
Arguments:
- hidden: bfloat16 [8192, 4096], P(('dp', 'sp')), parts along dimension 0
- w_q: bfloat16 [4096, 4096], replicated
- w_k: bfloat16 [4096, 1024], replicated
- w_v: bfloat16 [4096, 1024], replicated
- w_o: bfloat16 [4096, 4096], replicated
- expert_ids: int32 [8192, 2], P(('dp', 'sp')), parts along dimension 0
- router_probs: float32 [8192, 16], P(('dp', 'sp')), parts along dimension 0
Outputs:
- output 1: bfloat16 [8192, 4096], P(('dp', 'sp')), parts along dimension 0
- output 2: bfloat16 [64, 2048, 4096], P(('dp', 'sp')), parts along dimension 0
There are 4 independent parts. A program takes and returns all parts, laid end to end along the dimension named above; an argument that names none is the same for every part.
All inputs are finite; a program needn't handle non-finite values.
Results may differ from a plain program's by a relative error of at most 0.00968718.
Values are sent between devices in bfloat16 or wider.
A program may use at most 768 MiB of HBM per device.

v0:
```python
import functools
import math

import jax
import jax.numpy as jnp
from jax import lax
from jax.experimental import pallas as pl
from jax.experimental.pallas import tpu as pltpu
from jax.sharding import PartitionSpec as P

HEAD = 128
EXP2_SCALE = math.log2(math.e) / math.sqrt(HEAD)
MESH = pl.DeviceIdType.MESH
TILE = 512
SLOTS = 8
PER_TILE = TILE // HEAD
AHEAD = 3
VMEM_LIMIT = 67_000_000
VIA_NEXT = ((0, 1, 3, 4, 6, 7, 9, 10, 12, 13, 15), (0, 3, 6, 9, 12, 15), (2, 5, 8, 11, 14), (0, 1, 2, 4, 5, 6, 8, 9, 10, 12, 13, 14))
LAG = 3
OUT_SLOTS = 5
COLS = 512


def block_kernel(group, n_exp, x_hbm, wq, wk, wv, wo, ids_ref, probs_ref, h_all, meta_all,
                 xb, wbuf, kb, vb, q_s, acc, top_s, mass_s, keep_s, s_b, e_b, o_s, h_s, meta_s,
                 x_sem, w_sem, k_send, kr_l, kr_r, kr_o, kr_p, h_send, hr_l, hr_r, hr_o, hr_p, m_send, m_recv, m_loc):
    tok = xb.shape[0]
    chips = group // 2
    q_tiles = wq.shape[1] // TILE
    k_tiles = wk.shape[1] // TILE
    kv_tiles = 2 * k_tiles
    o_tiles = wo.shape[1] // TILE
    me = lax.axis_index("sp")
    core = lax.rem(me, 2)
    chip = lax.div(me, 2)
    right = lax.rem(me + 2, group)
    left = lax.rem(me + group - 2, group)
    partner = me + 1 - 2 * core
    opp = lax.rem(me + 4, group)
    last = chips - 1

    def remote(src, dst, send, recv, dev):
        return pltpu.make_async_remote_copy(src_ref=src, dst_ref=dst, send_sem=send, recv_sem=recv,
                                            device_id={"sp": dev}, device_id_type=MESH)

    def got(ref, sem):
        pltpu.make_async_copy(ref, ref, sem).wait()

    def w_copy(arr, col, slot):
        if not isinstance(col, int):
            col = pl.multiple_of(col, TILE)
        return pltpu.make_async_copy(arr.at[:, pl.ds(col, TILE)], wbuf.at[slot], w_sem.at[slot])

    x_copy = pltpu.make_async_copy(x_hbm, xb, x_sem)
    x_copy.start()
    w_copy(wk, 0, 0).start()

    barrier = pltpu.get_barrier_semaphore()
    for d in range(1, group):
        pl.semaphore_signal(barrier, inc=1, device_id={"sp": lax.rem(me + d, group)}, device_id_type=MESH)
    x_copy.wait()
    w_copy(wk, TILE, 1).start()

    sends_right = chip < last
    sends_left_k = chip == 0
    sends_left_v = chip < 2
    gets_left = chip > 0
    gets_right_k = chip == last
    fwd_k = (chip > 0) & (chip < last)
    gets_opp = chip >= 2

    def k_tile(p, carry):
        w_copy(wk, 0, p).wait()
        w_copy(wv, p * TILE, k_tiles + p).start()

        @pl.when(p == k_tiles - 1)
        def _():
            w_copy(wq, 0, kv_tiles).start()

        y = jnp.dot(xb[...], wbuf[p], preferred_element_type=jnp.float32).astype(jnp.bfloat16)
        for h in range(PER_TILE):
            kb[0, 0, p, h] = y[:, h * HEAD:(h + 1) * HEAD]

        @pl.when(p == 0)
        def _():
            pl.semaphore_wait(barrier, group - 1)

        src = kb.at[0, 0, p]

        @pl.when(sends_right)
        def _():
            remote(src, kb.at[3, 0, p], k_send.at[0], kr_l.at[p], right).start()

        @pl.when(sends_left_k)
        def _():
            remote(src, kb.at[1, 0, p], k_send.at[1], kr_r.at[p], left).start()

        @pl.when(core == 0)
        def _():
            remote(src, kb.at[0, 1, p], k_send.at[2], kr_p.at[0], partner).start()

        return carry

    lax.fori_loop(0, k_tiles, k_tile, 0)

    def v_tile(p, carry):
        w_copy(wv, 0, k_tiles + p).wait()
        w_copy(wq, (1 + p) * TILE, kv_tiles + 1 + p).start()
        y = jnp.dot(xb[...], wbuf[k_tiles + p], preferred_element_type=jnp.float32)
        for h in range(PER_TILE):
            vb[0, 0, p, h] = jnp.transpose(y[:, h * HEAD:(h + 1) * HEAD]).astype(jnp.bfloat16)
        src = vb.at[0, 0, p]

        @pl.when(sends_right)
        def _():
            remote(src, vb.at[3, 0, p], k_send.at[3], kr_l.at[k_tiles + p], right).start()

        @pl.when(sends_left_v)
        def _():
            remote(src, vb.at[1, 0, p], k_send.at[4], kr_r.at[k_tiles + p], left).start()

        @pl.when(core == 0)
        def _():
            remote(src, vb.at[0, 1, p], k_send.at[5], kr_p.at[4], partner).start()

        return carry

    lax.fori_loop(0, k_tiles, v_tile, 0)

    def q_tile(n, carry):
        slot = lax.rem(kv_tiles + n, SLOTS)
        w_copy(wq, 0, slot).wait()
        ahead = lax.rem(kv_tiles + AHEAD + n, SLOTS)

        @pl.when(n + AHEAD < q_tiles)
        def _():
            w_copy(wq, (n + AHEAD) * TILE, ahead).start()

        @pl.when(n + AHEAD >= q_tiles)
        def _():
            w_copy(wo, (n + AHEAD - q_tiles) * TILE, ahead).start()

        y = jnp.dot(xb[...], wbuf[slot], preferred_element_type=jnp.float32).astype(jnp.bfloat16)
        for h in range(PER_TILE):
            q_s[n, h] = y[:, h * HEAD:(h + 1) * HEAD]
        return carry

    lax.fori_loop(0, q_tiles, q_tile, 0)
    for n in range(AHEAD, o_tiles):
        w_copy(wo, n * TILE, (kv_tiles + q_tiles + n) % SLOTS).start()

    def k_partner(r, p):
        remote(kb.at[r, 0, p], kb.at[r, 1, p], k_send.at[5 + r], kr_p.at[r], partner).start()

    def v_partner(r, p):
        remote(vb.at[r, 0, p], vb.at[r, 1, p], k_send.at[8 + r], kr_p.at[4 + r], partner).start()

    @pl.when(gets_left)
    def _():
        for p in range(k_tiles):
            got(kb.at[3, 0, p], kr_l.at[p])

            @pl.when(fwd_k)
            def _():
                remote(kb.at[3, 0, p], kb.at[2, 0, p], k_send.at[12], kr_o.at[p], right).start()

            k_partner(3, p)

    expert = lax.broadcasted_iota(jnp.int32, (n_exp, tok), 0)
    hit0 = expert == ids_ref[0:1, :]
    hit1 = expert == ids_ref[1:2, :]
    probs = probs_ref[...]
    p0 = jnp.sum(jnp.where(hit0, probs, 0.0), axis=0, keepdims=True)
    p1 = jnp.sum(jnp.where(hit1, probs, 0.0), axis=0, keepdims=True)
    total = p0 + p1
    hits = hit0 | hit1
    before = (lax.broadcasted_iota(jnp.int32, (tok, tok), 0)
              < lax.broadcasted_iota(jnp.int32, (tok, tok), 1)).astype(jnp.float32).astype(jnp.bfloat16)
    earlier = jnp.dot(hits.astype(jnp.float32).astype(jnp.bfloat16), before, preferred_element_type=jnp.float32)
    meta_s[0:n_exp, :] = jnp.where(hits, earlier, -1.0)
    meta_s[n_exp:2 * n_exp, :] = jnp.where(hit0, p0 / total, jnp.where(hit1, p1 / total, 0.0))

    def attend(r, parts, lo=0, hi=None, first=False, diagonal=False):
        hi = q_tiles if hi is None else hi
        spare = q_tiles
        keys = parts * tok
        if diagonal:
            key_i = lax.broadcasted_iota(jnp.int32, (tok, tok), 0)
            row_i = lax.broadcasted_iota(jnp.int32, (tok, tok), 1)
            seen = row_i >= key_i

        def score(g, into, h, side):
            kp = lax.div(g, PER_TILE)
            kh = lax.rem(g, PER_TILE)
            q = q_s[g, h]
            top = None if first else top_s[g, h]
            old = top
            for o in range(parts):
                s = lax.dot_general(kb[r, o, kp, kh], q, (((1,), (1,)), ((), ())), preferred_element_type=jnp.float32)
                if diagonal and o == 0:
                    s = jnp.where(seen, s, -1e30)
                s_b[side, h, o] = s
                high = jnp.max(s, axis=0, keepdims=True)
                top = high if top is None else jnp.maximum(top, high)
            top_s[into, h] = top
            if not first:
                keep_s[into, h] = jnp.exp2((old - top) * EXP2_SCALE)

        def weigh(g, h, side):
            top = top_s[g, h]
            mass = None
            for o in range(parts):
                e = jnp.exp2((s_b[side, h, o] - top) * EXP2_SCALE)
                e_b[side, h, o * tok:(o + 1) * tok, :] = e.astype(jnp.bfloat16)
                part = jnp.sum(e, axis=0, keepdims=True)
                mass = part if mass is None else mass + part
            mass_s[g, h] = mass if first else mass + keep_s[g, h] * mass_s[g, h]

        def apply(g, into, h, side):
            kp = lax.div(g, PER_TILE)
            kh = lax.rem(g, PER_TILE)
            v = jnp.concatenate([vb[r, o, kp, kh] for o in range(parts)], axis=1)
            out = jnp.dot(v, e_b[side, h, 0:keys, :], preferred_element_type=jnp.float32)
            acc[into, h] = out if first else out + keep_s[into, h] * acc[into, h]

        def head_groups(i, carry):
            g = lo + 2 * i
            below = jnp.maximum(g - 1, lo)
            below_into = lax.select(g == lo, spare, g - 1)
            above = jnp.minimum(g + 2, hi - 1)
            above_into = lax.select(g == hi - 2, spare, g + 2)
            for h in range(PER_TILE):
                weigh(g, h, 0)
                score(g + 1, g + 1, h, 1)
                apply(below, below_into, h, 1)
            for h in range(PER_TILE):
                weigh(g + 1, h, 1)
                score(above, above_into, h, 0)
                apply(g, g, h, 0)
            return carry

        for h in range(PER_TILE):
            score(lo, lo, h, 0)
        lax.fori_loop(0, (hi - lo) // 2, head_groups, 0)
        for h in range(PER_TILE):
            apply(hi - 1, hi - 1, h, 1)

    for h in range(PER_TILE):
        e_b[1, h] = jnp.zeros((2 * tok, tok), jnp.bfloat16)
        acc[q_tiles, h] = jnp.zeros((HEAD, tok), jnp.float32)
        keep_s[q_tiles, h] = jnp.zeros((1, tok), jnp.float32)

    @pl.when(core == 0)
    def _():
        attend(0, 1, first=True, diagonal=True)

    @pl.when(core == 1)
    def _():
        got(kb.at[0, 1], kr_p.at[0])
        got(vb.at[0, 1], kr_p.at[4])
        attend(0, 2, first=True, diagonal=True)

    m_rows = meta_all.at[me]
    loc = pltpu.make_async_copy(meta_s, m_rows, m_loc)
    loc.start()
    for d in range(1, group):
        remote(meta_s, m_rows, m_send.at[d - 1], m_recv.at[d - 1], lax.rem(me + d, group)).start()

    def values_on_left():
        for p in range(k_tiles):
            got(vb.at[1, 0, p], kr_r.at[k_tiles + p])
            remote(vb.at[1, 0, p], vb.at[2, 0, p], k_send.at[13], kr_o.at[k_tiles + p], left).start()

    @pl.when(chip == last)
    def _():
        values_on_left()

    @pl.when(gets_left)
    def _():
        for p in range(k_tiles):
            got(vb.at[3, 0, p], kr_l.at[k_tiles + p])
            v_partner(3, p)

        @pl.when(gets_right_k)
        def _():
            for p in range(k_tiles):
                got(kb.at[1, 0, p], kr_r.at[p])
                k_partner(1, p)
                v_partner(1, p)

        got(kb.at[3, 1], kr_p.at[3])
        got(vb.at[3, 1], kr_p.at[7])
        attend(3, 2)

    def take_opp():
        for p in range(k_tiles):
            got(kb.at[2, 0, p], kr_o.at[p])
            k_partner(2, p)
            got(vb.at[2, 0, p], kr_o.at[k_tiles + p])
            v_partner(2, p)

    @pl.when(gets_right_k)
    def _():
        got(kb.at[1, 1], kr_p.at[1])
        got(vb.at[1, 1], kr_p.at[5])
        attend(1, 2, hi=q_tiles - 2)
        take_opp()
        attend(1, 2, lo=q_tiles - 2)

    @pl.when(gets_opp)
    def _():
        @pl.when(jnp.logical_not(gets_right_k))
        def _():
            take_opp()

        got(kb.at[2, 1], kr_p.at[2])
        got(vb.at[2, 1], kr_p.at[6])
        attend(2, 2)

    def finish(g, carry):
        for h in range(PER_TILE):
            o = jnp.transpose(acc[g, h] * (1.0 / mass_s[g, h]))
            o_s[:, pl.ds(pl.multiple_of(g * TILE + h * HEAD, HEAD), HEAD)] = o.astype(jnp.bfloat16)
        return carry

    lax.fori_loop(0, q_tiles, finish, 0)

    @pl.when(chip == 0)
    def _():
        got(kb.at[0, 0], k_send.at[1])
        got(vb.at[0, 0], k_send.at[4])
        values_on_left()

    def rows_of(dev):
        return pl.ds(pl.multiple_of(dev * tok, tok), tok)

    def piece(dev, n):
        col = n * TILE
        if not isinstance(col, int):
            col = pl.multiple_of(col, TILE)
        return h_all.at[rows_of(dev), pl.ds(col, TILE)]

    def to_left(n):
        remote(h_s.at[n], piece(me, n), h_send.at[1], hr_r.at[n], left).start()

    def o_tile(n, carry):
        slot = lax.rem(kv_tiles + q_tiles + n, SLOTS)
        w_copy(wo, 0, slot).wait()
        y = jnp.dot(o_s[...], wbuf[slot], preferred_element_type=jnp.float32)
        x = xb[:, pl.ds(pl.multiple_of(n * TILE, TILE), TILE)].astype(jnp.float32)
        h_s[n] = (x + y).astype(jnp.bfloat16)
        remote(h_s.at[n], piece(me, n), h_send.at[0], hr_l.at[n], right).start()

        @pl.when(chip > 0)
        def _():
            to_left(n)

        remote(h_s.at[n], piece(me, n), h_send.at[2], hr_p.at[0], partner).start()
        pltpu.make_async_copy(h_s.at[n], piece(me, n), x_sem).start()
        return carry

    lax.fori_loop(0, o_tiles, o_tile, 0)

    @pl.when(chip == 0)
    def _():
        got(vb.at[0, 0], k_send.at[13])
        for n in range(o_tiles):
            to_left(n)


    def of_chips(which):
        hit = jnp.bool_(False)
        for c in which:
            hit = hit | (chip == c)
        return hit

    halves = 2 * o_tiles
    on_right = [[m in VIA_NEXT[(c - 1) % chips] for m in range(halves)] for c in range(chips)]
    on_left = [[m not in VIA_NEXT[(c + 1) % chips] for m in range(halves)] for c in range(chips)]

    def half_piece(dev, m):
        return h_all.at[rows_of(dev), pl.ds(m * (TILE // 2), TILE // 2)]

    def from_left(n):
        got(piece(left, n), hr_l.at[n])
        for m in (2 * n, 2 * n + 1):
            @pl.when(of_chips([c for c in range(chips) if on_right[c][m]]))
            def _(m=m):
                remote(half_piece(left, m), half_piece(left, m), h_send.at[6], hr_o.at[m], right).start()

        remote(piece(left, n), piece(left, n), h_send.at[5], hr_p.at[3], partner).start()

    def from_right(n):
        got(piece(right, n), hr_r.at[n])
        for m in (2 * n, 2 * n + 1):
            @pl.when(of_chips([c for c in range(chips) if on_left[c][m]]))
            def _(m=m):
                remote(half_piece(right, m), half_piece(right, m), h_send.at[7], hr_o.at[m], left).start()

        remote(piece(right, n), piece(right, n), h_send.at[3], hr_p.at[1], partner).start()

    def in_turn(early, late):
        for n in range(o_tiles + LAG):
            if n < o_tiles:
                early(n)
            if n >= LAG:
                late(n - LAG)

    early_right = (chip == 0) | (chip == last)

    @pl.when(early_right)
    def _():
        in_turn(from_right, from_left)

    @pl.when(jnp.logical_not(early_right))
    def _():
        in_turn(from_left, from_right)

    for n in range(halves):
        got(half_piece(opp, n), hr_o.at[n])
        remote(half_piece(opp, n), half_piece(opp, n), h_send.at[4], hr_p.at[2], partner).start()

    mine = h_all.at[rows_of(me)]
    got(mine, x_sem)
    for i in range(6):
        got(mine, h_send.at[i])
    for c in range(chips):
        @pl.when(chip == c)
        def _():
            for i, on in ((6, on_right[c]), (7, on_left[c])):
                if sum(on):
                    got(h_all.at[rows_of(me), pl.ds(0, sum(on) * (TILE // 2))], h_send.at[i])
    for r in range(chips):
        got(h_all.at[rows_of(lax.rem(partner + 2 * r, group))], hr_p.at[r])
    k_own = kb.at[0, 0]
    v_own = vb.at[0, 0]
    for when, waits in ((sends_right, ((k_own, 0), (v_own, 3))), (chip == 1, ((v_own, 4),)),
                        (core == 0, ((k_own, 2), (v_own, 5))), (gets_left, ((k_own, 8), (v_own, 11))),
                        (gets_right_k, ((k_own, 6), (v_own, 9))), (gets_opp, ((k_own, 7), (v_own, 10))),
                        (fwd_k, ((k_own, 12),)), (chip == last, ((v_own, 13),))):
        @pl.when(when)
        def _(waits=waits):
            for ref, i in waits:
                got(ref, k_send.at[i])

    loc.wait()
    for d in range(1, group):
        got(meta_s, m_send.at[d - 1])
        got(meta_all.at[lax.rem(me + group - d, group)], m_recv.at[d - 1])


def dispatch_kernel(n_exp, own_exp, meta_ref, h_hbm, hid_hbm, buf_hbm, hb, ob, h_sem, o_sem, hid_sem):
    group, tok, width = hb.shape
    slots = ob.shape[0]
    me = lax.axis_index("sp")
    row = lax.broadcasted_iota(jnp.int32, (tok, tok), 0).astype(jnp.float32)

    def o_copy(s):
        rows = pl.ds(s * tok if isinstance(s, int) else pl.multiple_of(s * tok, tok), tok)
        return pltpu.make_async_copy(ob.at[lax.rem(s, slots)], buf_hbm.at[:, rows], o_sem.at[lax.rem(s, slots)])

    for s in range(group):
        pltpu.make_async_copy(h_hbm.at[pl.ds(s * tok, tok)], hb.at[s], h_sem.at[s]).start()

    def source(s, carry):
        pltpu.make_async_copy(hb.at[s], hb.at[s], h_sem.at[s]).wait()

        @pl.when(s == me)
        def _():
            pltpu.make_async_copy(hb.at[s], hid_hbm, hid_sem).start()

        @pl.when(s >= slots)
        def _():
            o_copy(s - slots).wait()

        picks, gates = [], []
        for e in range(own_exp):
            expert = me * own_exp + e
            pick = row == meta_ref[s, pl.ds(expert, 1), :]
            gates.append(jnp.sum(jnp.where(pick, meta_ref[s, pl.ds(n_exp + expert, 1), :], 0.0), axis=1, keepdims=True))
            picks.append(pick.astype(jnp.float32).astype(jnp.bfloat16))
        o = lax.rem(s, slots)
        for c in range(0, width, COLS):
            for e in range(own_exp):
                rows = jnp.dot(picks[e], hb[s, :, c:c + COLS], preferred_element_type=jnp.float32)
                ob[o, e, :, c:c + COLS] = (rows * gates[e]).astype(jnp.bfloat16)
        o_copy(s).start()
        return carry

    lax.fori_loop(0, group, source, 0)
    for s in range(group - slots, group):
        o_copy(s).wait()
    pltpu.make_async_copy(hb.at[0], hid_hbm, hid_sem).wait()


def solution(mesh):
    group = mesh.shape['sp']
    row_spec = P(('dp', 'sp'), None)
    buf_spec = P(('dp', 'sp'), None, None)

    def device_step(x_loc, w_q, w_k, w_v, w_o, ids_loc, probs_loc):
        tok, width = x_loc.shape
        n_exp = probs_loc.shape[1]
        own_exp = n_exp // group
        seq = tok * group
        q_tiles = w_q.shape[1] // TILE
        k_tiles = w_k.shape[1] // TILE
        chips = group // 2
        o_tiles = width // TILE
        bf16 = jnp.bfloat16
        any_spec = pl.BlockSpec(memory_space=pl.ANY)
        vmem_spec = pl.BlockSpec(memory_space=pltpu.VMEM)
        dma = pltpu.SemaphoreType.DMA
        h_all, meta_all = pl.pallas_call(
            functools.partial(block_kernel, group, n_exp),
            out_shape=(jax.ShapeDtypeStruct((seq, width), bf16),
                       jax.ShapeDtypeStruct((group, 2 * n_exp, tok), jnp.float32)),
            in_specs=[any_spec] * 5 + [vmem_spec] * 2,
            out_specs=(any_spec, any_spec),
            scratch_shapes=[
                pltpu.VMEM((tok, width), bf16),
                pltpu.VMEM((SLOTS, width, TILE), bf16),
                pltpu.VMEM((chips, 2, k_tiles, PER_TILE, tok, HEAD), bf16),
                pltpu.VMEM((chips, 2, k_tiles, PER_TILE, HEAD, tok), bf16),
                pltpu.VMEM((q_tiles, PER_TILE, tok, HEAD), bf16),
                pltpu.VMEM((q_tiles + 1, PER_TILE, HEAD, tok), jnp.float32),
                pltpu.VMEM((q_tiles + 1, PER_TILE, 1, tok), jnp.float32),
                pltpu.VMEM((q_tiles + 1, PER_TILE, 1, tok), jnp.float32),
                pltpu.VMEM((q_tiles + 1, PER_TILE, 1, tok), jnp.float32),
                pltpu.VMEM((2, PER_TILE, 2, tok, tok), jnp.float32),
                pltpu.VMEM((2, PER_TILE, 2 * tok, tok), bf16),
                pltpu.VMEM((tok, q_tiles * TILE), bf16),
                pltpu.VMEM((o_tiles, tok, TILE), bf16),
                pltpu.VMEM((2 * n_exp, tok), jnp.float32),
                dma, dma((SLOTS,)),
                dma((14,)), dma((2 * k_tiles,)), dma((2 * k_tiles,)), dma((2 * k_tiles,)), dma((2 * chips,)),
                dma((8,)), dma((o_tiles,)), dma((o_tiles,)), dma((2 * o_tiles,)), dma((chips,)),
                dma((group - 1,)), dma((group - 1,)), dma,
            ],
            compiler_params=pltpu.CompilerParams(collective_id=0, has_side_effects=True,
                                                 vmem_limit_bytes=VMEM_LIMIT),
            name="block",
        )(x_loc, w_q, w_k, w_v, w_o, ids_loc.T, probs_loc.T)

        hidden_out, buf = pl.pallas_call(
            functools.partial(dispatch_kernel, n_exp, own_exp),
            out_shape=(jax.ShapeDtypeStruct((tok, width), bf16),
                       jax.ShapeDtypeStruct((own_exp, seq, width), bf16)),
            in_specs=[vmem_spec, any_spec],
            out_specs=(any_spec, any_spec),
            scratch_shapes=[pltpu.VMEM((group, tok, width), bf16), pltpu.VMEM((OUT_SLOTS, own_exp, tok, width), bf16),
                            dma((group,)), dma((OUT_SLOTS,)), dma],
            compiler_params=pltpu.CompilerParams(vmem_limit_bytes=VMEM_LIMIT),
            name="dispatch",
        )(meta_all, h_all)
        return hidden_out, buf

    return jax.shard_map(device_step, mesh=mesh,
                         in_specs=(row_spec, P(), P(), P(), P(), row_spec, row_spec),
                         out_specs=(row_spec, buf_spec), check_vma=False)
```

profile of v0, /device:TPU:81, one launch (start us, length us, event | category | flops | bytes accessed | tf_op | source)
XLA Modules:
  0.0 139.4 jit_solution(9436696374369317956)
XLA Ops:
  0.6 121.4 %block.1 = (bf16[2048,4096]{1,0:T(8,128)(2,1)}, f32[8,32,256]{2,1,0:T(8,128)}) custom-call(bf16[256,4096]{1,0:T(8,128)(2,1)} %x_hbm.1, bf16[4096,4096]{1,0:T(8,128)(2,1)} %wq.1, bf16[4096,1024]{1,0:T(8,128)(2,1)} %wk.1, bf16[4096,1024]{1,0:T(8,128)(2,1)} %wv.1, bf16[4096,4096]{1,0:T(8,128)(2,1)} %wo.1, s32[2,256]{1,0:T(2,128)} %bitcast.3, f32[16,256]{1,0:T(8,128)} %bitcast.2), custom_call_target="tpu_custom_call" | custom-call | tf_op jit(solution)/shard_map/block/pallas_call | solution.py:515
  122.1 17.2 %dispatch.1 = (bf16[256,4096]{1,0:T(8,128)(2,1)}, bf16[2,2048,4096]{2,1,0:T(8,128)(2,1)}) custom-call(f32[8,32,256]{2,1,0:T(8,128)} %get-tuple-element.4.meta_ref, bf16[2048,4096]{1,0:T(8,128)(2,1)} %get-tuple-element.5.h_hbm), custom_call_target="tpu_custom_call" | custom-call | tf_op jit(solution)/shard_map/dispatch/pallas_call | solution.py:546
where the time goes:
time: 140 us; the launch traced here: 139 us
  Pallas kernels  139 us (99%)
    pallas_call x1, Pallas kernels, device_step(): pl.pallas_call(functools.partial(block_kernel, group, n_exp), out_shape=(...  121 us
    pallas_call x1, Pallas kernels, device_step(): pl.pallas_call(functools.partial(dispatch_kernel, n_exp, own_exp), out_sh...  17.2 us

commit v1 on v0

--- a/solution.py
+++ b/solution.py
@@ -460,11 +460,22 @@
         rows = pl.ds(s * tok if isinstance(s, int) else pl.multiple_of(s * tok, tok), tok)
         return pltpu.make_async_copy(ob.at[lax.rem(s, slots)], buf_hbm.at[:, rows], o_sem.at[lax.rem(s, slots)])
 
-    for s in range(group):
-        pltpu.make_async_copy(h_hbm.at[pl.ds(s * tok, tok)], hb.at[s], h_sem.at[s]).start()
+    def read(sources):
+        for s in sources:
+            pltpu.make_async_copy(h_hbm.at[pl.ds(s * tok, tok)], hb.at[s], h_sem.at[s]).start()
+
+    read(range(2))
 
     def source(s, carry):
         pltpu.make_async_copy(hb.at[s], hb.at[s], h_sem.at[s]).wait()
+
+        @pl.when(s == 0)
+        def _():
+            read(range(2, 5))
+
+        @pl.when(s == 1)
+        def _():
+            read(range(5, group))
 
         @pl.when(s == me)
         def _():

time: 140 us -> 140 us (level)
  no operation moved by 1% of the time
where the time goes in v1:
time: 140 us
  Pallas kernels  139 us (99%)
    pallas_call x1, Pallas kernels, device_step(): pl.pallas_call(functools.partial(block_kernel, group, n_exp), out_shape=(...  121 us
    pallas_call x1, Pallas kernels, device_step(): pl.pallas_call(functools.partial(dispatch_kernel, n_exp, own_exp), out_sh...  17.6 us

profile of v1, /device:TPU:81, one launch (start us, length us, event | category | flops | bytes accessed | tf_op | source)
XLA Modules:
  0.0 139.9 jit_solution(6607560090026330736)
XLA Ops:
  0.6 121.4 %block.1 = (bf16[2048,4096]{1,0:T(8,128)(2,1)}, f32[8,32,256]{2,1,0:T(8,128)}) custom-call(bf16[256,4096]{1,0:T(8,128)(2,1)} %x_hbm.1, bf16[4096,4096]{1,0:T(8,128)(2,1)} %wq.1, bf16[4096,1024]{1,0:T(8,128)(2,1)} %wk.1, bf16[4096,1024]{1,0:T(8,128)(2,1)} %wv.1, bf16[4096,4096]{1,0:T(8,128)(2,1)} %wo.1, s32[2,256]{1,0:T(2,128)} %bitcast.3, f32[16,256]{1,0:T(8,128)} %bitcast.2), custom_call_target="tpu_custom_call" | custom-call | tf_op jit(solution)/shard_map/block/pallas_call | solution.py:526
  122.1 17.6 %dispatch.1 = (bf16[256,4096]{1,0:T(8,128)(2,1)}, bf16[2,2048,4096]{2,1,0:T(8,128)(2,1)}) custom-call(f32[8,32,256]{2,1,0:T(8,128)} %get-tuple-element.4.meta_ref, bf16[2048,4096]{1,0:T(8,128)(2,1)} %get-tuple-element.5.h_hbm), custom_call_target="tpu_custom_call" | custom-call | tf_op jit(solution)/shard_map/dispatch/pallas_call | solution.py:557
